TPU v7x, 128 devices: a whole 4x4x4 slice. The times are simulated.
128 devices in a mesh: data: 1, tp: 2 (over core), ep: 64 (over z, y, x).
Axes of the slice: x: 4, y: 4, z: 4, core: 2. Of those that a mesh axis runs over, the one named last changes fastest.
Arguments:
- tokens: bfloat16 [24576, 2048], P(('data', 'ep', 'tp'))
- expert_ids: int32 [24576, 6], P(('data', 'ep', 'tp'))
- gate_vals: float32 [24576, 6], P(('data', 'ep', 'tp'))
- slot_ids: int32 [24576, 6], P(('data', 'ep', 'tp'))
- send_counts: int32 [128, 64], P(('data', 'ep', 'tp'))
- shared_w1: bfloat16 [2048, 2816], P(None, 'tp')
- shared_w3: bfloat16 [2048, 2816], P(None, 'tp')
- shared_w2: bfloat16 [2816, 2048], P('tp')
- expert_w1: bfloat16 [64, 2048, 1408], P('ep')
- expert_w3: bfloat16 [64, 2048, 1408], P('ep')
- expert_w2: bfloat16 [64, 1408, 2048], P('ep')
Outputs:
- output: bfloat16 [24576, 2048], P(('data', 'ep', 'tp'))
All inputs are finite; a program needn't handle non-finite values.
Results may differ from a plain program's by a relative error of at most 0.00129.
Values are sent between devices in bfloat16 or wider.
A program may use at most 1 GiB of HBM per device.

v0:
```python
import jax
import jax.numpy as jnp
from jax import lax
from jax.sharding import PartitionSpec as P

CAP_FACTOR = 4


def capacity_rows(n_tok, top_k, n_exp):
    return min(n_tok, ((CAP_FACTOR * n_tok * top_k // n_exp + 7) // 8) * 8)


def solution(mesh):
    ep_size = mesh.shape["ep"]
    row_spec = P(("data", "ep", "tp"), None)
    expert_spec = P("ep", None, None)

    def layer_body(tokens, expert_ids, gate_vals, slot_ids, send_counts, shared_w1, shared_w3, shared_w2, expert_w1, expert_w3, expert_w2):
        n_tok, d_model = tokens.shape
        top_k = expert_ids.shape[1]
        n_local = expert_w1.shape[0]
        n_exp = n_local * ep_size
        capacity = capacity_rows(n_tok, top_k, n_exp)
        n_rows = n_exp * capacity

        gathered = lax.all_gather(tokens, "tp", axis=0, tiled=True)
        pre_gate = jnp.dot(gathered, shared_w1, preferred_element_type=jnp.float32)
        pre_up = jnp.dot(gathered, shared_w3, preferred_element_type=jnp.float32)
        shared_hidden = (jax.nn.silu(pre_gate) * pre_up).astype(jnp.bfloat16)
        part_sum = jnp.dot(shared_hidden, shared_w2, preferred_element_type=jnp.float32)
        shared_out = lax.psum_scatter(part_sum, "tp", scatter_dimension=0, tiled=True)

        row_limit = jnp.take(send_counts[0], expert_ids, axis=0)
        kept_mask = (slot_ids >= 0) & (slot_ids < row_limit)
        dest_row = jnp.where(kept_mask, expert_ids * capacity + slot_ids, n_rows)
        tok_ids = jnp.broadcast_to(jnp.arange(n_tok, dtype=jnp.int32)[:, None], (n_tok, top_k)).reshape(-1)
        owner_ids = jnp.full((n_rows,), n_tok, jnp.int32).at[dest_row.reshape(-1)].set(tok_ids, mode="drop")
        send_buf = jnp.take(tokens, owner_ids, axis=0, mode="fill", fill_value=0)
        send_buf = send_buf.reshape(ep_size, n_local, capacity, d_model)
        recv_buf = lax.all_to_all(send_buf, "ep", 0, 2, tiled=True)
        recv_buf = recv_buf.reshape(n_local, ep_size * capacity, d_model)

        exp_gate = jnp.einsum("erd,edf->erf", recv_buf, expert_w1, preferred_element_type=jnp.float32)
        exp_up = jnp.einsum("erd,edf->erf", recv_buf, expert_w3, preferred_element_type=jnp.float32)
        exp_hidden = (jax.nn.silu(exp_gate) * exp_up).astype(jnp.bfloat16)
        exp_out = jnp.einsum("erf,efd->erd", exp_hidden, expert_w2, preferred_element_type=jnp.float32).astype(jnp.bfloat16)
        back_buf = lax.all_to_all(exp_out.reshape(1, n_local, ep_size * capacity, d_model), "ep", 2, 0, tiled=True)

        back_rows = back_buf.reshape(n_rows, d_model)
        picked = jnp.take(back_rows, dest_row, axis=0, mode="fill", fill_value=0)
        gate_eff = jnp.where(kept_mask, gate_vals, 0.0)
        routed_sum = jnp.sum(gate_eff[:, :, None] * picked.astype(jnp.float32), axis=1)
        return (tokens.astype(jnp.float32) + shared_out + routed_sum).astype(jnp.bfloat16)

    return jax.shard_map(
        layer_body,
        mesh=mesh,
        in_specs=(row_spec, row_spec, row_spec, row_spec, row_spec, P(None, "tp"), P(None, "tp"), P("tp", None), expert_spec, expert_spec, expert_spec),
        out_specs=row_spec,
        check_vma=False,
    )
```

profile of v0, /device:TPU:2, one launch (start us, length us, event | category | flops | bytes accessed | tf_op | source)
XLA Modules:
  0.0 1114.2 jit_solution(6195981891054914660)
XLA Ops:
  6.5 0.7 compare_select_fusion.3
  7.6 7.0 gather_fusion
  15.9 6.5 scatter_custom_fusion
  22.5 18.3 %gather_fusion.1 = bf16[4608,2048]{1,0:T(8,128)(2,1)} fusion(bf16[192,2048]{1,0:T(8,128)(2,1)S(1)} %copy-done.2, s32[5120]{0:T(1024)S(1)} %pad_clamp_fusion), kind=kCustom, calls=%fused_computation.1 | custom fusion | bytes 37767168 | tf_op jit(solution)/shard_map/jit(_take)/gather | solution.py:38
  40.8 9.5 broadcast_select_fusion
  50.3 254.7 %all_to_all.8 = bf16[64,1,72,2048]{3,2,1,0:T(8,128)(2,1)S(1)} all-to-all(bf16[64,1,72,2048]{3,2,1,0:T(8,128)(2,1)S(1)} %broadcast_select_fusion), channel_id=1, replica_groups=mesh['data'=1,'tp'=2,'ep'=64] {'ep'}, dimensions={0} | all-to-all | bytes 37748736 | tf_op jit(solution)/shard_map/all_to_all | solution.py:40
  305.0 6.5 copy-done.4
  311.5 35.2 %fusion.4 = f32[4608,1408]{1,0:T(8,128)} fusion(bf16[4608,2048]{1,0:T(8,128)(2,1)S(1)} %bitcast.45, bf16[1,2048,1408]{2,1,0:T(8,128)(2,1)} %param.19), kind=kOutput, calls=%fused_computation.12 | convolution fusion | flops 26575110144 | bytes 50593792 | tf_op jit(solution)/shard_map/erd,edf->erf/dot_general | solution.py:43
  346.7 39.5 %multiply_convert_fusion.clone.4 = bf16[4608,1408]{1,0:T(8,128)(2,1)} fusion(f32[4608,1408]{1,0:T(8,128)} %fusion.4, bf16[4608,2048]{1,0:T(8,128)(2,1)} %bitcast.46, bf16[1,2048,1408]{2,1,0:T(8,128)(2,1)} %param.20), kind=kOutput, calls=%fused_computation.4.clone.clone.clone.1 | convolution fusion | flops 26614038528 | bytes 63569920 | tf_op jit(solution)/shard_map/erd,edf->erf/dot_general | solution.py:44
  386.2 32.3 %fusion = bf16[1,1,4608,2048]{3,2,1,0:T(8,128)(2,1)S(1)} fusion(bf16[1,1408,2048]{2,1,0:T(8,128)(2,1)S(1)} %bitcast.48, bf16[4608,1408]{1,0:T(8,128)(2,1)} %multiply_convert_fusion.clone.4), kind=kOutput, calls=%fused_computation.8 | convolution fusion | flops 26584547328 | bytes 37617664 | tf_op jit(solution)/shard_map/erf,efd->erd/dot_general | solution.py:46
  418.6 33.4 %copy.66 = bf16[1,1,4608,2048]{3,1,0,2:T(2,128)(2,1)} copy(bf16[1,1,4608,2048]{3,2,1,0:T(8,128)(2,1)S(1)} %fusion) | data formatting | bytes 37748736 | tf_op jit(solution)/shard_map/reshape | solution.py:47
  452.4 114.2 %reduce.2 = bf16[4608,2048]{1,0:T(8,128)(2,1)} reduce(bf16[4608,1,1,2048]{3,2,1,0:T(2,128)(2,1)} %bitcast.42, bf16[]{:T(256)} %broadcast.57), dimensions={1,2}, to_apply=%bitcast.39.reduce_sub_computation | reduce | bytes 37748736
  566.7 49.4 %reshape.160 = bf16[64,2,73728]{2,1,0:T(2,128)(2,1)} reshape(bf16[4608,2048]{1,0:T(8,128)(2,1)} %reduce.2) | data formatting | bytes 37748736
  616.1 30.9 %all-to-all-start.1 = ((bf16[64,2,73728]{2,1,0:T(2,128)(2,1)}), bf16[64,2,73728]{2,1,0:T(2,128)(2,1)}, u32[]{:S(2)}, u32[]{:S(2)}) async-start(bf16[64,2,73728]{2,1,0:T(2,128)(2,1)} %reshape.160), calls=%async_computation.2 | async-start | bytes 37748736 | tf_op jit(solution)/shard_map/all_to_all | solution.py:47
  647.8 15.4 %all-gather.2.cloned.1.call-done = bf16[384,2048]{1,0:T(8,128)(2,1)} async-done(((bf16[192,2048]{1,0:T(8,128)(2,1)}), bf16[384,2048]{1,0:T(8,128)(2,1)}) %all-gather.2.cloned.1.call-update) | async-done | bytes 1572880 | tf_op jit(solution)/shard_map/all_gather | solution.py:26
  663.2 7.2 fusion.15
  670.4 11.7 %fusion.7 = f32[384,2048]{1,0:T(8,128)} fusion(bf16[1408,2048]{1,0:T(8,128)(2,1)} %param.18, bf16[384,2048]{1,0:T(8,128)(2,1)S(1)} %copy-done.12, bf16[2048,1408]{1,0:T(8,128)(2,1)} %param.17, f32[384,1408]{1,0:T(8,128)} %fusion.15), kind=kOutput, calls=%fused_computation.17 | convolution fusion | flops 4432429056 | bytes 18415616 | tf_op jit(solution)/shard_map/dot_general | solution.py:30
  682.8 310.9 %all-to-all-done.1 = bf16[64,2,73728]{2,1,0:T(2,128)(2,1)} async-done(((bf16[64,2,73728]{2,1,0:T(2,128)(2,1)}), bf16[64,2,73728]{2,1,0:T(2,128)(2,1)}, u32[]{:S(2)}, u32[]{:S(2)}) %all-to-all-start.1) | async-done | bytes 18874400 | tf_op jit(solution)/shard_map/all_to_all | solution.py:47
  993.7 47.8 %reshape.161 = bf16[4608,1,1,2048]{3,2,1,0:T(2,128)(2,1)} reshape(bf16[64,2,73728]{2,1,0:T(2,128)(2,1)} %all-to-all-done.1) | data formatting | bytes 37748736
  1041.5 26.8 %copy.65 = bf16[1,1,4608,2048]{3,2,0,1:T(8,128)(2,1)} copy(bf16[1,1,4608,2048]{3,1,0,2:T(2,128)(2,1)} %bitcast.43) | data formatting | bytes 37748736
  1068.3 19.5 %gather_fusion.2 = bf16[1152,2048]{1,0:T(8,128)(2,1)} fusion(bf16[4608,2048]{1,0:T(8,128)(2,1)} %bitcast.41, s32[2048]{0:T(1024)S(1)} %pad_clamp_fusion.1), kind=kCustom, calls=%fused_computation.2 | custom fusion | bytes 9441792 | tf_op jit(solution)/shard_map/jit(_take)/gather | solution.py:50
  1087.7 8.5 reshape.137
  1096.2 8.3 multiply_reduce_fusion
  1104.5 2.7 add_convert_fusion
  (58 shorter events, 3.6 us)
Async XLA Ops:
  6.5 1.0 copy-start
  7.5 7.2 copy-start.7
  7.6 7.2 copy-start.10
  14.5 8.0 copy-start.2
  15.4 25.4 %copy-start.5 = (s32[192,6]{0,1:T(8,128)}, s32[192,6]{0,1:T(8,128)S(1)}, u32[]{:S(2)}) copy-start(s32[192,6]{0,1:T(8,128)S(1)} %get-tuple-element.6) | copy-start | bytes 13828
  305.0 6.5 copy-start.4
  311.5 74.8 %slice-start = ((s8[5767168]{0:T(1024)(128)(4,1)}), s8[1572864]{0:T(1024)(128)(4,1)S(1)}, s32[]{:S(2)}) async-start(s8[5767168]{0:T(1024)(128)(4,1)} %bitcast.47), calls=%async_computation.5 | async-start | bytes 3145728
  346.7 39.5 %slice-start.1 = ((s8[5767168]{0:T(1024)(128)(4,1)}), s8[4194304]{0:T(1024)(128)(4,1)S(1)}, s32[]{:S(2)}) async-start(s8[5767168]{0:T(1024)(128)(4,1)} %bitcast.47), calls=%async_computation.6 | async-start | bytes 8388608
  616.1 377.6 %all-to-all-start.1 = ((bf16[64,2,73728]{2,1,0:T(2,128)(2,1)}), bf16[64,2,73728]{2,1,0:T(2,128)(2,1)}, u32[]{:S(2)}, u32[]{:S(2)}) async-start(bf16[64,2,73728]{2,1,0:T(2,128)(2,1)} %reshape.160), calls=%async_computation.2 | async-start | bytes 37748736 | tf_op jit(solution)/shard_map/all_to_all | solution.py:47
  647.0 16.2 %all-gather.2.cloned.1.call-start = ((), (), s32[]{:S(2)}) async-start(), calls=%async_computation.3 | async-start | bytes 2359296 | tf_op jit(solution)/shard_map/all_gather | solution.py:26
  647.7 456.8 %reduce-scatter.2.cloned.1.call-start = ((), (), s32[]{:S(2)}) async-start(), calls=%async_computation.4 | async-start | bytes 4718592 | tf_op jit(solution)/shard_map/reduce_scatter | solution.py:31
  663.2 7.2 copy-start.12
  670.4 11.8 %copy-start.6 = (s32[192,6]{0,1:T(8,128)S(1)}, s32[192,6]{0,1:T(8,128)}, u32[]{:S(2)}) copy-start(s32[192,6]{0,1:T(8,128)} %copy-done.5) | copy-start | bytes 13828
  670.4 12.1 %copy-start.8 = (pred[192,6]{0,1:T(8,128)(4,1)S(1)}, pred[192,6]{0,1:T(8,128)(4,1)}, u32[]{:S(2)}) copy-start(pred[192,6]{0,1:T(8,128)(4,1)} %get-tuple-element.7) | copy-start | bytes 3460
  670.4 12.1 %copy-start.9 = (f32[192,6]{0,1:T(8,128)S(1)}, f32[192,6]{0,1:T(8,128)}, u32[]{:S(2)}) copy-start(f32[192,6]{0,1:T(8,128)} %param.13) | copy-start | bytes 13828
  670.4 12.2 %copy-start.11 = (pred[192,6]{0,1:T(8,128)(4,1)S(1)}, pred[192,6]{0,1:T(8,128)(4,1)}, u32[]{:S(2)}) copy-start(pred[192,6]{0,1:T(8,128)(4,1)} %get-tuple-element.5) | copy-start | bytes 3460
  1087.7 19.5 %copy-start.1 = (s32[1,64]{1,0:T(1,128)S(1)}, s32[1,64]{1,0:T(1,128)}, u32[]{:S(2)}) copy-start(s32[1,64]{1,0:T(1,128)} %param.15) | copy-start | bytes 772
  1096.2 8.3 copy-start.3
Sparse Core Ops, SparseCore 0:
  649.4 13.7 all-gather.1
  682.3 14.1 reduce-scatter.1
where the time goes:
time: 1110 us
  waiting for transfers between devices  327 us (29%)
  blocking collectives  255 us (23%)
  local copies, waits for them, and re-layouts  226 us (20%)
  other arithmetic  136 us (12%)
  matrix products  126 us (11%)
  starting transfers between devices  31 us (3%)
  between operations  13.9 us (1%)
    all_to_all x1, waiting for transfers between devices, layer_body(): lax.all_to_all(exp_out.reshape(1, n_local, ep_size * capacity, d_model),...  311 us
    all_to_all x1, blocking collectives, layer_body(): recv_buf = lax.all_to_all(send_buf, 'ep', 0, 2, tiled=True)  255 us
    unnamed x34, local copies, waits for them, and re-layouts  131 us
    unnamed x2, other arithmetic  114 us
    dot_general x1, matrix products, layer_body(): jnp.einsum('erd,edf->erf', recv_buf, expert_w3, preferred_element_type=jn...  39.5 us
    dot_general x1, matrix products, layer_body(): jnp.einsum('erd,edf->erf', recv_buf, expert_w1, preferred_element_type=jn...  35.2 us
    reshape x1, local copies, waits for them, and re-layouts, layer_body(): exp_out.reshape(1, n_local, ep_size * capacity, d_model)  33.4 us
    dot_general x1, matrix products, layer_body(): jnp.einsum('erf,efd->erd', exp_hidden, expert_w2, preferred_element_type=...  32.3 us
  transfers between devices with their start and end apart: 3, of which 2 were waited for; matrix products, arithmetic and copies ran while one was open for 12% of the time, Pallas kernels for 0%

commit v1 on v0

v1 whole, which is shorter than its diff:
```python
import functools

import jax
import jax.numpy as jnp
from jax import lax
from jax.experimental import pallas as pl
from jax.experimental.pallas import tpu as pltpu
from jax.sharding import PartitionSpec as P

CAP_FACTOR = 4
SIDE = 4
GROUPS = SIDE * SIDE
UNIT = 8
LAGS = (1, 4, 7)


def capacity_rows(n_tok, top_k, n_exp):
    return min(n_tok, ((CAP_FACTOR * n_tok * top_k // n_exp + 7) // 8) * 8)


def swiglu(rows, w1, w3, w2):
    gate = jnp.dot(rows, w1, preferred_element_type=jnp.float32)
    up = jnp.dot(rows, w3, preferred_element_type=jnp.float32)
    hidden = (jax.nn.silu(gate) * up).astype(jnp.bfloat16)
    return jnp.dot(hidden, w2, preferred_element_type=jnp.float32)


def bf16_parts(weights):
    parts, rest = [], weights
    for _ in range(3):
        part = lax.reduce_precision(rest, 8, 7)
        rest = rest - part
        parts.append(part.astype(jnp.bfloat16))
    return parts


def expert_kernel(n_items, rows, w1, w3, w2, hop1, hop2, out, in_buf, out_buf, load_sem, send_sem, recv_sem, own_sem):
    me = lax.axis_index("ep")
    coords = (lax.rem(me, SIDE), lax.rem(me // SIDE, SIDE), me // GROUPS)
    bufs = (out_buf, hop1, hop2, out)

    def part(color, phase, item, at):
        buf = bufs[phase]
        if phase == 0 and color == 2:
            return buf.at[item, at]
        if (phase == 0 and color == 1) or (phase == 1 and color == 1):
            return buf.at[item, :, at]
        return buf.at[item, :, :, at]

    def start(phase, item):
        for color in range(3):

            @pl.when(lax.rem(item, 3) == color)
            def _():
                axis = (color + phase) % 3
                mine, before = coords[axis], coords[(axis + 2) % 3]
                kept, own = own_sem.at[item, phase], out_buf.at[item]
                if phase == 0:
                    pltpu.make_async_copy(part(color, 0, item, mine), hop1.at[item, mine], kept).start()
                elif phase == 1:
                    pltpu.make_async_copy(part(color, 1, item, mine), own.at[0], kept).start()
                else:
                    pltpu.make_async_copy(own.at[0, :, mine], own.at[1, before], kept).start()
                    for e in range(1, SIDE):
                        src = lax.rem(before + e, SIDE)
                        pltpu.make_async_copy(hop2.at[item, src, :, mine], own.at[1, src], kept).start()
                for d in (1, 3, 2):
                    to = lax.rem(mine + d, SIDE)
                    chip = [to if axis == i else coords[i] for i in range(3)]

                    def send(src_ref, dst_ref):
                        pltpu.make_async_remote_copy(
                            src_ref=src_ref,
                            dst_ref=dst_ref,
                            send_sem=send_sem.at[item, phase, d - 1],
                            recv_sem=recv_sem.at[item, phase, d - 1],
                            device_id={"ep": (chip[2] * SIDE + chip[1]) * SIDE + chip[0]},
                            device_id_type=pl.DeviceIdType.MESH,
                        ).start()

                    if phase < 2:
                        send(part(color, phase, item, to), bufs[phase + 1].at[item, mine])
                    else:
                        send(own.at[0, :, to], out.at[item, mine, before])
                        for e in range(1, SIDE):
                            src = lax.rem(before + e, SIDE)
                            send(hop2.at[item, src, :, to], out.at[item, mine, src])

    def wait(phase, item):
        block = bufs[phase + 1].at[item, 0]
        pltpu.make_async_copy(block, block, own_sem.at[item, phase]).wait()
        for d in range(3):
            pltpu.make_async_remote_copy(
                src_ref=block,
                dst_ref=block,
                send_sem=send_sem.at[item, phase, d],
                recv_sem=recv_sem.at[item, phase, d],
                device_id={"ep": lax.rem(me + 1, GROUPS * SIDE)},
                device_id_type=pl.DeviceIdType.MESH,
            ).wait()

    def load(item, slot):
        return pltpu.make_async_copy(rows.at[:, pl.ds(item * UNIT, UNIT)], in_buf.at[slot], load_sem.at[slot])

    load(0, 0).start()

    def body(t, _):
        @pl.when(t < n_items)
        def _():
            slot = lax.rem(t, 2)

            @pl.when(t + 1 < n_items)
            def _():
                load(t + 1, 1 - slot).start()

            load(t, slot).wait()

        def exchange():
            for phase, lag in enumerate(LAGS):
                item = t - lag

                @pl.when((item >= 0) & (item < n_items))
                def _():
                    if phase > 0:
                        wait(phase - 1, item)
                    start(phase, item)

        @pl.when(t < n_items)
        def _():
            slot = lax.rem(t, 2)
            n_src, _, d_model = in_buf.shape[1:]
            x = in_buf[slot].astype(jnp.float32).reshape(n_src * UNIT, d_model).astype(jnp.bfloat16)
            gate = jnp.dot(x, w1[...], preferred_element_type=jnp.float32)
            up = jnp.dot(x, w3[...], preferred_element_type=jnp.float32)
            hidden = (gate * jax.nn.sigmoid(gate) * up).astype(jnp.bfloat16)
            exchange()
            res = jnp.dot(hidden, w2[...], preferred_element_type=jnp.float32)
            out_buf[t] = res.reshape(SIDE, SIDE, SIDE, UNIT, d_model).astype(jnp.bfloat16)

        @pl.when(t >= n_items)
        def _():
            exchange()

        return 0

    lax.fori_loop(0, n_items + LAGS[2], body, 0)

    def finish(item, _):
        wait(2, item)
        for color in range(3):

            @pl.when(lax.rem(item, 3) == color)
            def _():
                pltpu.make_async_copy(out_buf.at[item, 1], out.at[item, coords[(color + 2) % 3]], own_sem.at[item, 2]).start()

        return 0

    lax.fori_loop(0, n_items, finish, 0)

    def done(item, _):
        pltpu.make_async_copy(out_buf.at[item, 1], out.at[item, 0], own_sem.at[item, 2]).wait()
        return 0

    lax.fori_loop(0, n_items, done, 0)


def solution(mesh):
    ep_size = mesh.shape["ep"]
    row_spec = P(("data", "ep", "tp"), None)
    expert_spec = P("ep", None, None)

    def layer_body(tokens, expert_ids, gate_vals, slot_ids, send_counts, shared_w1, shared_w3, shared_w2, expert_w1, expert_w3, expert_w2):
        n_tok, d_model = tokens.shape
        top_k = expert_ids.shape[1]
        n_exp = ep_size
        d_ff = expert_w1.shape[2]
        cap = capacity_rows(n_tok, top_k, n_exp)
        n_rows = n_exp * cap
        swap = [(0, 1), (1, 0)]

        gathered = lax.all_gather(tokens, "ep", axis=0, tiled=True).reshape(ep_size, n_tok, d_model)

        is_exp = expert_ids[:, :, None] == jnp.arange(n_exp, dtype=jnp.int32)
        row_limit = jnp.sum(jnp.where(is_exp, send_counts[0], 0), axis=2)
        kept = (slot_ids >= 0) & (slot_ids < row_limit)
        is_slot = kept[:, :, None] & (slot_ids[:, :, None] == jnp.arange(cap, dtype=jnp.int32))
        tok_nums = jnp.arange(1, n_tok + 1, dtype=jnp.float32)[:, None, None]
        owners = jnp.einsum("tje,tjr->er", jnp.where(is_exp, tok_nums, 0.0).astype(jnp.bfloat16), is_slot.astype(jnp.bfloat16), preferred_element_type=jnp.float32)
        owners = lax.all_to_all(owners, "ep", 0, 0, tiled=True).astype(jnp.int32)
        other = lax.ppermute(tokens, "tp", swap)
        part = swiglu(jnp.concatenate([tokens, other], axis=0), shared_w1, shared_w3, shared_w2)
        shared_out = part[:n_tok] + lax.ppermute(part[n_tok:], "tp", swap)

        n_items = cap // UNIT
        item = slot_ids // UNIT
        ex, ey, ez = expert_ids % SIDE, expert_ids // SIDE % SIDE, expert_ids // GROUPS
        place = jnp.where(item % 3 == 0, (ez * SIDE + ey) * SIDE + ex, jnp.where(item % 3 == 1, (ex * SIDE + ez) * SIDE + ey, (ey * SIDE + ex) * SIDE + ez))
        dest = jnp.where(kept, (item * n_exp + place) * UNIT + slot_ids % UNIT, -1)
        row_nums = jnp.arange(n_rows, dtype=jnp.int32)
        weights = jnp.zeros((n_tok, n_rows), jnp.float32)
        for j in range(top_k):
            weights = weights + jnp.where(dest[:, j : j + 1] == row_nums[None, :], gate_vals[:, j : j + 1], 0.0)
        weights = lax.optimization_barrier(jnp.concatenate(bf16_parts(weights), axis=0))

        pick = owners.reshape(ep_size, cap)[:, :, None] == jnp.arange(1, n_tok + 1, dtype=jnp.int32)
        rows = jnp.einsum("srt,std->srd", pick.astype(jnp.bfloat16), gathered, preferred_element_type=jnp.float32).astype(jnp.bfloat16)
        vmem = pl.BlockSpec(memory_space=pltpu.VMEM)
        hbm = pl.BlockSpec(memory_space=pl.ANY)
        boxes = (n_items, SIDE, SIDE, SIDE, UNIT, d_model)
        back = pl.pallas_call(
            functools.partial(expert_kernel, n_items),
            name="expert_return",
            out_shape=[jax.ShapeDtypeStruct(boxes, jnp.bfloat16)] * 3,
            in_specs=[hbm, vmem, vmem, vmem],
            out_specs=[hbm] * 3,
            scratch_shapes=[
                pltpu.VMEM((2, ep_size, UNIT, d_model), jnp.bfloat16),
                pltpu.VMEM(boxes, jnp.bfloat16),
                pltpu.SemaphoreType.DMA((2,)),
                pltpu.SemaphoreType.DMA((n_items, 3, 3)),
                pltpu.SemaphoreType.DMA((n_items, 3, 3)),
                pltpu.SemaphoreType.DMA((n_items, 3)),
            ],
            compiler_params=pltpu.CompilerParams(has_side_effects=True, vmem_limit_bytes=66_000_000),
            cost_estimate=pl.CostEstimate(flops=6 * n_rows * d_model * d_ff, bytes_accessed=n_rows * d_model * 6, transcendentals=n_rows * d_ff),
        )(rows, expert_w1[0], expert_w3[0], expert_w2[0])[2].reshape(n_rows, d_model)
        routed = jnp.dot(weights, back, preferred_element_type=jnp.float32)
        routed = routed[:n_tok] + routed[n_tok : 2 * n_tok] + routed[2 * n_tok :]
        return (tokens.astype(jnp.float32) + shared_out + routed).astype(jnp.bfloat16)

    return jax.shard_map(
        layer_body,
        mesh=mesh,
        in_specs=(row_spec, row_spec, row_spec, row_spec, row_spec, P(None, "tp"), P(None, "tp"), P("tp", None), expert_spec, expert_spec, expert_spec),
        out_specs=row_spec,
        check_vma=False,
    )
```

time: 1110 us -> 545 us (0.49)
  the two profiles are of different devices: /device:TPU:2 before, /device:TPU:1 now
where the time goes in v1:
time: 545 us; the launch traced here: 544 us
  Pallas kernels  264 us (48%)
  waiting for transfers between devices  179 us (33%)
  matrix products  57.6 us (11%)
  between operations  13.5 us (2%)
  starting transfers between devices  13 us (2%)
  other arithmetic  12.2 us (2%)
    pallas_call x1, Pallas kernels, layer_body(): pl.pallas_call(functools.partial(expert_kernel, n_items), name='expert_re...  264 us
    all_gather x1, waiting for transfers between devices, layer_body(): lax.all_gather(tokens, 'ep', axis=0, tiled=True)  178 us
    dot_general x1, matrix products, layer_body(): jnp.einsum('srt,std->srd', pick.astype(jnp.bfloat16), gathered, preferred...  23.3 us
    dot_general x1, matrix products, layer_body(): routed = jnp.dot(weights, back, preferred_element_type=jnp.float32)  15.7 us
    all_to_all x1, starting transfers between devices, layer_body(): owners = lax.all_to_all(owners, 'ep', 0, 0, tiled=True).astype(jnp.int32)  11.3 us
  transfers between devices with their start and end apart: 4, of which 1 were waited for; matrix products, arithmetic and copies ran while one was open for 13% of the time, Pallas kernels for 49%

profile of v1, /device:TPU:1, one launch (start us, length us, event | category | flops | bytes accessed | tf_op | source)
XLA Modules:
  0.0 544.2 jit_solution(14660747553482649338)
XLA Ops:
  6.5 0.7 all-gather.2.cloned.1.call-update
  7.3 1.4 collective-permute-start
  8.7 0.9 select_reduce_fusion
  9.6 0.8 fusion.21
  10.3 1.6 fusion.11
  11.9 11.3 %all-to-all-start = ((f32[64,1,72]{2,1,0:T(1,128)}), f32[64,1,72]{2,1,0:T(1,128)S(1)}, u32[]{:S(2)}, u32[]{:S(2)}) async-start(f32[64,1,72]{2,1,0:T(1,128)} %bitcast.15), calls=%async_computation | async-start | bytes 65536 | tf_op jit(solution)/shard_map/all_to_all | solution.py:189
  23.2 0.9 fusion.28
  24.1 1.2 constant_dynamic-update-slice_fusion.1
  25.3 4.6 reduce-precision_convert_fusion.1
  29.9 2.8 pad_maximum_fusion
  32.7 0.0 all-to-all-done
  32.7 0.0 collective-permute-done
  32.7 0.1 constant_dynamic-update-slice_fusion
  32.8 1.2 copy-done.3
  34.0 6.6 %fusion.31 = f32[384,1408]{1,0:T(8,128)} fusion(bf16[384,2048]{1,0:T(8,128)(2,1)S(1)} %constant_dynamic-update-slice_fusion, bf16[2048,1408]{1,0:T(8,128)(2,1)} %param.16), kind=kOutput, calls=%fused_computation.75 | convolution fusion | flops 2214592512 | bytes 9502720 | tf_op jit(solution)/shard_map/dot_general | solution.py:22
  40.5 10.5 %fusion.8 = f32[384,2048]{1,0:T(8,128)S(1)} fusion(bf16[1408,2048]{1,0:T(8,128)(2,1)} %param.18, f32[384,1408]{1,0:T(8,128)} %fusion.31, bf16[384,2048]{1,0:T(8,128)(2,1)} %copy-done.3, bf16[2048,1408]{1,0:T(8,128)(2,1)} %param.17), kind=kOutput, calls=%fused_computation.25 | convolution fusion | flops 4432429056 | bytes 18415616 | tf_op jit(solution)/shard_map/dot_general | solution.py:25
  51.0 1.4 slice.69
  52.4 0.3 collective-permute-start.1
  52.7 178.4 %all-gather.2.cloned.1.call-done = bf16[12288,2048]{1,0:T(8,128)(2,1)} async-done(((bf16[192,2048]{1,0:T(8,128)(2,1)}), bf16[12288,2048]{1,0:T(8,128)(2,1)}) %all-gather.2.cloned.1.call-update) | async-done | bytes 50331664 | tf_op jit(solution)/shard_map/all_gather | solution.py:181
  231.1 23.3 %convolution_convert_fusion.rows = bf16[64,72,2048]{2,1,0:T(8,128)(2,1)} fusion(bf16[64,192,2048]{2,1,0:T(8,128)(2,1)} %bitcast.31, s32[192]{0:T(256)S(1)} %iota_add_fusion, s32[64,72]{1,0:T(8,128)S(1)} %bitcast.32), kind=kOutput, calls=%fused_computation | convolution fusion | flops 3634200576 | bytes 69225216 | tf_op jit(solution)/shard_map/srt,std->srd/dot_general | solution.py:206
  254.4 264.0 %expert_return.1 = (bf16[9,4,4,4,8,2048]{5,4,3,2,1,0:T(8,128)(2,1)}, bf16[9,4,4,4,8,2048]{5,4,3,2,1,0:T(8,128)(2,1)}, bf16[9,4,4,4,8,2048]{5,4,3,2,1,0:T(8,128)(2,1)}) custom-call(bf16[64,72,2048]{2,1,0:T(8,128)(2,1)} %convolution_convert_fusion.rows, bf16[2048,1408]{1,0:T(8,128)(2,1)} %bitcast.46, bf16[2048,1408]{1,0:T(8,128)(2,1)} %bitcast.47, ...), custom_call_target="tpu_custom_call" | custom-call | flops 79725330432 | bytes 56623104 | tf_op jit(solution)/shard_map/expert_return/pallas_call | solution.py:210
  518.4 0.0 copy-start
  518.4 15.7 %fusion.32 = f32[576,2048]{1,0:T(8,128)S(1)} fusion(bf16[576,4608]{1,0:T(8,128)(2,1)} %pad_maximum_fusion, bf16[4608,2048]{1,0:T(8,128)(2,1)} %bitcast.49), kind=kOutput, calls=%fused_computation.76 | convolution fusion | flops 10871635968 | bytes 28901376 | tf_op jit(solution)/shard_map/dot_general | solution.py:227
  534.2 3.2 fusion.6
  (12 shorter events, 0.1 us)
Async XLA Ops:
  6.5 224.6 %all-gather.2.cloned.1.call-start = ((), (), s32[]{:S(2)}) async-start(), calls=%async_computation.1 | async-start | bytes 51118080 | tf_op jit(solution)/shard_map/all_gather | solution.py:181
  7.3 25.4 %collective-permute-start = (bf16[192,2048]{1,0:T(8,128)(2,1)}, bf16[192,2048]{1,0:T(8,128)(2,1)S(1)}, u32[]{:S(2)}, u32[]{:S(2)}) collective-permute-start(bf16[192,2048]{1,0:T(8,128)(2,1)} %param.11), channel_id=1, source_target_pairs={{0,64},{64,0},{1,65},{65,1},{2,66},{66,2},{3,67},{67,3},{4,68},{68... | collective-permute-start | bytes 2359304 | tf_op jit(solution)/shard_map/ppermute | solution.py:190
  11.9 20.8 %all-to-all-start = ((f32[64,1,72]{2,1,0:T(1,128)}), f32[64,1,72]{2,1,0:T(1,128)S(1)}, u32[]{:S(2)}, u32[]{:S(2)}) async-start(f32[64,1,72]{2,1,0:T(1,128)} %bitcast.15), calls=%async_computation | async-start | bytes 65536 | tf_op jit(solution)/shard_map/all_to_all | solution.py:189
  32.8 1.2 copy-start.3
  51.0 203.4 %copy-start.1 = (f32[384,2048]{1,0:T(8,128)}, f32[384,2048]{1,0:T(8,128)S(1)}, u32[]{:S(2)}) copy-start(f32[384,2048]{1,0:T(8,128)S(1)} %fusion.8) | copy-start | bytes 9437188
  52.4 481.7 %collective-permute-start.1 = (f32[192,2048]{1,0:T(8,128)}, f32[192,2048]{1,0:T(8,128)}, u32[]{:S(2)}, u32[]{:S(2)}) collective-permute-start(f32[192,2048]{1,0:T(8,128)} %slice.69), channel_id=1, source_target_pairs={{0,64},{64,0},{1,65},{65,1},{2,66},{66,2},{3,67},{67,3},{4,68},{68... | collective-permute-start | bytes 4718600 | tf_op jit(solution)/shard_map/ppermute | solution.py:192
  518.4 15.8 %copy-start = (bf16[192,2048]{1,0:T(8,128)(2,1)S(1)}, bf16[192,2048]{1,0:T(8,128)(2,1)}, u32[]{:S(2)}) copy-start(bf16[192,2048]{1,0:T(8,128)(2,1)} %param.11) | copy-start | bytes 2359300
  518.4 15.8 %copy-start.2 = (f32[384,2048]{1,0:T(8,128)S(1)}, f32[384,2048]{1,0:T(8,128)}, u32[]{:S(2)}) copy-start(f32[384,2048]{1,0:T(8,128)} %copy-done.1) | copy-start | bytes 9437188
Sparse Core Ops, SparseCore 0:
  10.1 221.0 all-gather.1

commit v2 on v1

v2 whole, which is shorter than its diff:
```python
import functools

import jax
import jax.numpy as jnp
from jax import lax
from jax.experimental import pallas as pl
from jax.experimental.pallas import tpu as pltpu
from jax.sharding import PartitionSpec as P

CAP_FACTOR = 4
SIDE = 4
GROUPS = SIDE * SIDE
UNIT = 8
LAGS = (0, 2, 4, 5, 6, 9, 12)


def capacity_rows(n_tok, top_k, n_exp):
    return min(n_tok, ((CAP_FACTOR * n_tok * top_k // n_exp + 7) // 8) * 8)


def swiglu(rows, w1, w3, w2):
    gate = jnp.dot(rows, w1, preferred_element_type=jnp.float32)
    up = jnp.dot(rows, w3, preferred_element_type=jnp.float32)
    hidden = (jax.nn.silu(gate) * up).astype(jnp.bfloat16)
    return jnp.dot(hidden, w2, preferred_element_type=jnp.float32)


def bf16_parts(weights):
    parts, rest = [], weights
    for _ in range(3):
        part = lax.reduce_precision(rest, 8, 7)
        rest = rest - part
        parts.append(part.astype(jnp.bfloat16))
    return parts


def expert_kernel(n_items, packed, w1, w3, w2, out1, out2, came, back1, back2, back, in_buf, out_buf, load_sem, send_sem, recv_sem, own_sem):
    me = lax.axis_index("ep")
    coords = (lax.rem(me, SIDE), lax.rem(me // SIDE, SIDE), me // GROUPS)
    away, home = (packed, out1, out2, came), (out_buf, back1, back2, back)

    def start(way, phase, item):
        bufs = (away, home)[way]
        for color in range(3):

            @pl.when(lax.rem(item, 3) == color)
            def _():
                axis = (color + phase) % 3
                mine, before = coords[axis], coords[(axis + 2) % 3]
                kept, own = own_sem.at[way, item, phase], out_buf.at[item]
                if phase == 0:
                    pieces = [(lambda at: bufs[0].at[item, :, :, at], None)]
                elif way == 1 and phase == 1:
                    pieces = [(lambda at: bufs[1].at[item, :, :, at], None)]
                else:
                    held = own.at[phase - 1 - way]
                    pieces = [(lambda at, held=held: held.at[:, at], before)]
                    for e in range(1, SIDE):
                        src = lax.rem(before + e, SIDE)
                        pieces.append((lambda at, src=src: bufs[phase].at[item, src, :, at], src))
                if way == 1 and phase == 0:
                    stay = bufs[1].at[item, mine]
                else:
                    stay = own.at[phase - way]
                for piece, place in pieces:
                    pltpu.make_async_copy(piece(mine), stay if place is None else stay.at[place], kept).start()
                for d in (1, 3, 2):
                    to = lax.rem(mine + d, SIDE)
                    chip = [to if axis == i else coords[i] for i in range(3)]
                    for piece, place in pieces:
                        box = bufs[phase + 1].at[item, mine]
                        pltpu.make_async_remote_copy(
                            src_ref=piece(to),
                            dst_ref=box if place is None else box.at[place],
                            send_sem=send_sem.at[way, item, phase, d - 1],
                            recv_sem=recv_sem.at[way, item, phase, d - 1],
                            device_id={"ep": (chip[2] * SIDE + chip[1]) * SIDE + chip[0]},
                            device_id_type=pl.DeviceIdType.MESH,
                        ).start()

    def wait(way, phase, item):
        block = (away, home)[way][phase + 1].at[item, 0]
        pltpu.make_async_copy(block, block, own_sem.at[way, item, phase]).wait()
        for d in range(3):
            pltpu.make_async_remote_copy(
                src_ref=block,
                dst_ref=block,
                send_sem=send_sem.at[way, item, phase, d],
                recv_sem=recv_sem.at[way, item, phase, d],
                device_id={"ep": lax.rem(me + 1, GROUPS * SIDE)},
                device_id_type=pl.DeviceIdType.MESH,
            ).wait()

    def load(item, slot):
        for color in range(3):

            @pl.when(lax.rem(item, 3) == color)
            def _():
                mine = coords[(color + 2) % 3]
                pltpu.make_async_copy(out_buf.at[item, 2], in_buf.at[slot, mine], load_sem.at[slot]).start()
                for e in range(1, SIDE):
                    src = lax.rem(mine + e, SIDE)
                    pltpu.make_async_copy(came.at[item, src], in_buf.at[slot, src], load_sem.at[slot]).start()

    def first(item, _):
        start(0, 0, item)
        return 0

    lax.fori_loop(0, n_items, first, 0)

    def at_step(t, lag, act):
        item = t - lag

        @pl.when((item >= 0) & (item < n_items))
        def _():
            act(item)

    def body(t, _):
        def middle(item):
            wait(0, 0, item)
            start(0, 1, item)

        def arrive(item):
            wait(0, 1, item)
            start(0, 2, item)

        def fetch(item):
            wait(0, 2, item)
            load(item, lax.rem(item, 2))

        at_step(t, LAGS[0], middle)
        at_step(t, LAGS[1], arrive)
        at_step(t, LAGS[2], fetch)

        def exchange():
            for phase in range(3):

                def go(item, phase=phase):
                    if phase > 0:
                        wait(1, phase - 1, item)
                    start(1, phase, item)

                at_step(t, LAGS[4 + phase], go)

        now = t - LAGS[3]
        busy = (now >= 0) & (now < n_items)

        @pl.when(busy)
        def _():
            slot = lax.rem(now, 2)
            d_model = in_buf.shape[-1]
            pltpu.make_async_copy(came.at[now], in_buf.at[slot], load_sem.at[slot]).wait()
            x = in_buf[slot].astype(jnp.float32).reshape(SIDE**3 * UNIT, d_model).astype(jnp.bfloat16)
            gate = jnp.dot(x, w1[...], preferred_element_type=jnp.float32)
            up = jnp.dot(x, w3[...], preferred_element_type=jnp.float32)
            hidden = (gate * jax.nn.sigmoid(gate) * up).astype(jnp.bfloat16)
            exchange()
            res = jnp.dot(hidden, w2[...], preferred_element_type=jnp.float32)
            out_buf[now] = res.reshape(SIDE, SIDE, SIDE, UNIT, d_model).astype(jnp.bfloat16)

        @pl.when(jnp.logical_not(busy))
        def _():
            exchange()

        return 0

    lax.fori_loop(0, n_items + LAGS[6], body, 0)

    def finish(item, _):
        wait(1, 2, item)
        for color in range(3):

            @pl.when(lax.rem(item, 3) == color)
            def _():
                pltpu.make_async_copy(out_buf.at[item, 1], back.at[item, coords[(color + 2) % 3]], own_sem.at[1, item, 2]).start()

        return 0

    lax.fori_loop(0, n_items, finish, 0)

    def done(item, _):
        pltpu.make_async_copy(out_buf.at[item, 1], back.at[item, 0], own_sem.at[1, item, 2]).wait()
        return 0

    lax.fori_loop(0, n_items, done, 0)


def solution(mesh):
    ep_size = mesh.shape["ep"]
    row_spec = P(("data", "ep", "tp"), None)
    expert_spec = P("ep", None, None)

    def layer_body(tokens, expert_ids, gate_vals, slot_ids, send_counts, shared_w1, shared_w3, shared_w2, expert_w1, expert_w3, expert_w2):
        n_tok, d_model = tokens.shape
        top_k = expert_ids.shape[1]
        n_exp = ep_size
        d_ff = expert_w1.shape[2]
        cap = capacity_rows(n_tok, top_k, n_exp)
        n_rows = n_exp * cap
        swap = [(0, 1), (1, 0)]

        is_exp = expert_ids[:, :, None] == jnp.arange(n_exp, dtype=jnp.int32)
        row_limit = jnp.sum(jnp.where(is_exp, send_counts[0], 0), axis=2)
        kept = (slot_ids >= 0) & (slot_ids < row_limit)

        other = lax.ppermute(tokens, "tp", swap)
        part = swiglu(jnp.concatenate([tokens, other], axis=0), shared_w1, shared_w3, shared_w2)
        shared_out = part[:n_tok] + lax.ppermute(part[n_tok:], "tp", swap)

        n_items = cap // UNIT
        item = slot_ids // UNIT
        ex, ey, ez = expert_ids % SIDE, expert_ids // SIDE % SIDE, expert_ids // GROUPS
        place = jnp.where(item % 3 == 0, (ez * SIDE + ey) * SIDE + ex, jnp.where(item % 3 == 1, (ex * SIDE + ez) * SIDE + ey, (ey * SIDE + ex) * SIDE + ez))
        dest = jnp.where(kept, (item * n_exp + place) * UNIT + slot_ids % UNIT, -1)
        row_nums = jnp.arange(n_rows, dtype=jnp.int32)
        weights = jnp.zeros((n_tok, n_rows), jnp.float32)
        sel = jnp.zeros((n_tok, n_rows), jnp.bool_)
        for j in range(top_k):
            here = dest[:, j : j + 1] == row_nums[None, :]
            sel = sel | here
            weights = weights + jnp.where(here, gate_vals[:, j : j + 1], 0.0)
        weights = lax.optimization_barrier(jnp.concatenate(bf16_parts(weights), axis=0))

        boxes = (n_items, SIDE, SIDE, SIDE, UNIT, d_model)
        packed = lax.dot_general(sel.astype(jnp.bfloat16), tokens, (((0,), (0,)), ((), ())), preferred_element_type=jnp.float32)
        packed = packed.astype(jnp.bfloat16).reshape(boxes)
        vmem = pl.BlockSpec(memory_space=pltpu.VMEM)
        hbm = pl.BlockSpec(memory_space=pl.ANY)
        back = pl.pallas_call(
            functools.partial(expert_kernel, n_items),
            name="expert_exchange",
            out_shape=[jax.ShapeDtypeStruct(boxes, jnp.bfloat16)] * 6,
            in_specs=[hbm, vmem, vmem, vmem],
            out_specs=[hbm] * 6,
            scratch_shapes=[
                pltpu.VMEM((2,) + boxes[1:], jnp.bfloat16),
                pltpu.VMEM(boxes, jnp.bfloat16),
                pltpu.SemaphoreType.DMA((2,)),
                pltpu.SemaphoreType.DMA((2, n_items, 3, 3)),
                pltpu.SemaphoreType.DMA((2, n_items, 3, 3)),
                pltpu.SemaphoreType.DMA((2, n_items, 3)),
            ],
            compiler_params=pltpu.CompilerParams(has_side_effects=True, vmem_limit_bytes=66_000_000),
            cost_estimate=pl.CostEstimate(flops=6 * n_rows * d_model * d_ff, bytes_accessed=n_rows * d_model * 6, transcendentals=n_rows * d_ff),
        )(packed, expert_w1[0], expert_w3[0], expert_w2[0])[5].reshape(n_rows, d_model)
        routed = jnp.dot(weights, back, preferred_element_type=jnp.float32)
        routed = routed[:n_tok] + routed[n_tok : 2 * n_tok] + routed[2 * n_tok :]
        return (tokens.astype(jnp.float32) + shared_out + routed).astype(jnp.bfloat16)

    return jax.shard_map(
        layer_body,
        mesh=mesh,
        in_specs=(row_spec, row_spec, row_spec, row_spec, row_spec, P(None, "tp"), P(None, "tp"), P("tp", None), expert_spec, expert_spec, expert_spec),
        out_specs=row_spec,
        check_vma=False,
    )
```

time: 545 us -> 494 us (0.906)
  waiting for transfers between devices: 179 us -> 0.01 us
  Pallas kernels: 264 us -> 434 us
  matrix products: 57.6 us -> 42.3 us
  between operations: 13.5 us -> 0.13 us
  starting transfers between devices: 13 us -> 4.52 us
    all_gather x1 -> x0, waiting for transfers between devices: 178 us -> none  [layer_body(): lax.all_gather(tokens, 'ep', axis=0, tiled=True)]
    pallas_call x1, Pallas kernels: 264 us -> 434 us  [layer_body(): pl.pallas_call(functools.partial(expert_kernel, n_items), name='expert_ex...]
    dot_general x2 -> x1, matrix products: 24.8 us -> 12.1 us  [layer_body(): lax.dot_general(sel.astype(jnp.bfloat16), tokens, (((0,), (0,)), ((), ())...]
    all_to_all x1 -> x0, starting transfers between devices: 11.3 us -> none  [layer_body(): owners = lax.all_to_all(owners, 'ep', 0, 0, tiled=True).astype(jnp.int32)]
  transfers between devices with their start and end apart: 4 -> 2, of which waited for: 1 -> 0; matrix products, arithmetic and copies ran while one was open for 13% -> 8% of each run, Pallas kernels for 49% -> 88%
where the time goes in v2:
time: 494 us
  Pallas kernels  434 us (88%)
  matrix products  42.3 us (9%)
  other arithmetic  10.8 us (2%)
    pallas_call x1, Pallas kernels, layer_body(): pl.pallas_call(functools.partial(expert_kernel, n_items), name='expert_ex...  434 us
    dot_general x1, matrix products, layer_body(): routed = jnp.dot(weights, back, preferred_element_type=jnp.float32)  15.7 us
    dot_general x1, matrix products, layer_body(): lax.dot_general(sel.astype(jnp.bfloat16), tokens, (((0,), (0,)), ((), ())...  12.1 us
    dot_general x1, matrix products, swiglu(): return jnp.dot(hidden, w2, preferred_element_type=jnp.float32)  10.5 us
  transfers between devices with their start and end apart: 2, of which 0 were waited for; matrix products, arithmetic and copies ran while one was open for 8% of the time, Pallas kernels for 88%

profile of v2, /device:TPU:1, one launch (start us, length us, event | category | flops | bytes accessed | tf_op | source)
XLA Modules:
  0.0 493.9 jit_solution(8172090272844491296)
XLA Ops:
  0.0 1.4 collective-permute-start
  1.4 0.9 select_reduce_fusion
  2.2 0.8 fusion.22
  3.0 0.9 fusion.28
  3.9 12.1 %convolution_convert_fusion = bf16[4608,2048]{1,0:T(8,128)(2,1)} fusion(bf16[192,2048]{1,0:T(8,128)(2,1)} %param.11, s32[192]{0:T(256)S(1)} %bitcast.28, s32[192]{0:T(256)S(1)} %bitcast.30, s32[192]{0:T(256)S(1)} %bitcast.32, s32[192]{0:T(256)S(1)} %bitcast.34, s32[192]{0:T(256)S(1)} %bitcast.36, s32[192]{0:T(256)S(1)} %bitcast.26), kind=kOutput, calls=%fused_computation | convolution fusion | flops 3643047936 | bytes 19665408 | tf_op jit(solution)/shard_map/dot_general | solution.py:225
  16.0 433.8 %expert_exchange.1 = (bf16[9,4,4,4,8,2048]{5,4,3,2,1,0:T(8,128)(2,1)}, bf16[9,4,4,4,8,2048]{5,4,3,2,1,0:T(8,128)(2,1)}, bf16[9,4,4,4,8,2048]{5,4,3,2,1,0:T(8,128...) custom-call(bf16[9,4,4,4,8,2048]{5,4,3,2,1,0:T(8,128)(2,1)} %bitcast, ...), custom_call_target="tpu_custom_call" | custom-call | flops 79725330432 | bytes 56623104 | tf_op jit(solution)/shard_map/expert_exchange/pallas_call | solution.py:229
  449.8 0.0 slice-start
  449.8 4.6 reduce-precision_convert_fusion.1
  454.4 0.0 copy-start
  454.4 0.0 slice-start.1
  454.5 2.8 pad_maximum_fusion
  457.3 0.1 constant_dynamic-update-slice_fusion.1
  457.4 0.0 collective-permute-done
  457.4 0.1 constant_dynamic-update-slice_fusion
  457.5 1.1 copy-done.2
  458.6 0.0 slice-done
  458.6 4.1 fusion.31
  462.7 10.5 %fusion.17 = f32[384,2048]{1,0:T(8,128)S(1)} fusion(bf16[1408,2048]{1,0:T(8,128)(2,1)} %param.18, f32[384,1408]{1,0:T(8,128)} %fusion.31, bf16[384,2048]{1,0:T(8,128)(2,1)} %copy-done.2, bf16[2048,1408]{1,0:T(8,128)(2,1)} %param.17), kind=kOutput, calls=%fused_computation.33 | convolution fusion | flops 4432429056 | bytes 18415616 | tf_op jit(solution)/shard_map/dot_general | solution.py:25
  473.2 0.1 slice.69
  473.3 3.2 collective-permute-start.1
  476.4 15.7 %fusion.32 = f32[576,2048]{1,0:T(8,128)S(1)} fusion(bf16[576,4608]{1,0:T(8,128)(2,1)} %pad_maximum_fusion, bf16[4608,2048]{1,0:T(8,128)(2,1)} %bitcast.50), kind=kOutput, calls=%fused_computation.71 | convolution fusion | flops 10871635968 | bytes 28901376 | tf_op jit(solution)/shard_map/dot_general | solution.py:246
  492.1 0.0 collective-permute-done.1
  492.1 0.0 copy-done.1
  492.1 1.8 fusion.15
  (6 shorter events, 0.0 us)
Async XLA Ops:
  0.0 457.4 %collective-permute-start = (bf16[192,2048]{1,0:T(8,128)(2,1)}, bf16[192,2048]{1,0:T(8,128)(2,1)S(1)}, u32[]{:S(2)}, u32[]{:S(2)}) collective-permute-start(bf16[192,2048]{1,0:T(8,128)(2,1)} %param.11), channel_id=1, source_target_pairs={{0,64},{64,0},{1,65},{65,1},{2,66},{66,2},{3,67},{67,3},{4,68},{68... | collective-permute-start | bytes 2359304 | tf_op jit(solution)/shard_map/ppermute | solution.py:206
  449.8 8.8 %slice-start = ((s8[5767168]{0:T(1024)(128)(4,1)}), s8[4194304]{0:T(1024)(128)(4,1)S(1)}, s32[]{:S(2)}) async-start(s8[5767168]{0:T(1024)(128)(4,1)} %bitcast.48), calls=%async_computation | async-start | bytes 8388608
  454.4 2.9 copy-start
  454.4 4.2 slice-start.1
  457.5 1.1 copy-start.2
  473.3 18.8 %collective-permute-start.1 = (f32[192,2048]{1,0:T(8,128)S(1)}, f32[192,2048]{1,0:T(8,128)S(1)}, u32[]{:S(2)}, u32[]{:S(2)}) collective-permute-start(f32[192,2048]{1,0:T(8,128)S(1)} %slice.69), channel_id=1, source_target_pairs={{0,64},{64,0},{1,65},{65,1},{2,66},{66,2},{3,67},{67,3},{4,68},{68... | collective-permute-start | bytes 4718600 | tf_op jit(solution)/shard_map/ppermute | solution.py:208
  476.4 15.7 %copy-start.1 = (bf16[192,2048]{1,0:T(8,128)(2,1)S(1)}, bf16[192,2048]{1,0:T(8,128)(2,1)}, u32[]{:S(2)}) copy-start(bf16[192,2048]{1,0:T(8,128)(2,1)} %param.11) | copy-start | bytes 2359300

commit v3 on v2

--- a/solution.py
+++ b/solution.py
@@ -11,7 +11,7 @@
 SIDE = 4
 GROUPS = SIDE * SIDE
 UNIT = 8
-LAGS = (0, 2, 4, 5, 6, 9, 12)
+LAGS = (0, 3, 5, 6, 7, 9, 11)
 
 
 def capacity_rows(n_tok, top_k, n_exp):
@@ -34,10 +34,10 @@
     return parts
 
 
-def expert_kernel(n_items, packed, w1, w3, w2, out1, out2, came, back1, back2, back, in_buf, out_buf, load_sem, send_sem, recv_sem, own_sem):
+def expert_kernel(n_items, toks, dest, w1_hbm, w3_hbm, w2_hbm, out1, out2, came, back1, back2, back, in_buf, out_buf, w1, w3, w2, load_sem, send_sem, recv_sem, own_sem, weight_sem):
     me = lax.axis_index("ep")
     coords = (lax.rem(me, SIDE), lax.rem(me // SIDE, SIDE), me // GROUPS)
-    away, home = (packed, out1, out2, came), (out_buf, back1, back2, back)
+    away, home = (out_buf, out1, out2, came), (out_buf, back1, back2, back)
 
     def start(way, phase, item):
         bufs = (away, home)[way]
@@ -48,20 +48,15 @@
                 axis = (color + phase) % 3
                 mine, before = coords[axis], coords[(axis + 2) % 3]
                 kept, own = own_sem.at[way, item, phase], out_buf.at[item]
-                if phase == 0:
-                    pieces = [(lambda at: bufs[0].at[item, :, :, at], None)]
-                elif way == 1 and phase == 1:
-                    pieces = [(lambda at: bufs[1].at[item, :, :, at], None)]
+                if phase < 2:
+                    pieces = [(lambda at: bufs[phase].at[item, :, :, at], None)]
                 else:
-                    held = own.at[phase - 1 - way]
+                    held = own.at[0]
                     pieces = [(lambda at, held=held: held.at[:, at], before)]
                     for e in range(1, SIDE):
                         src = lax.rem(before + e, SIDE)
                         pieces.append((lambda at, src=src: bufs[phase].at[item, src, :, at], src))
-                if way == 1 and phase == 0:
-                    stay = bufs[1].at[item, mine]
-                else:
-                    stay = own.at[phase - way]
+                stay = bufs[1].at[item, mine] if phase == 0 else own.at[phase - 1]
                 for piece, place in pieces:
                     pltpu.make_async_copy(piece(mine), stay if place is None else stay.at[place], kept).start()
                 for d in (1, 3, 2):
@@ -97,16 +92,37 @@
             @pl.when(lax.rem(item, 3) == color)
             def _():
                 mine = coords[(color + 2) % 3]
-                pltpu.make_async_copy(out_buf.at[item, 2], in_buf.at[slot, mine], load_sem.at[slot]).start()
+                pltpu.make_async_copy(out_buf.at[item, 1], in_buf.at[slot, mine], load_sem.at[slot]).start()
                 for e in range(1, SIDE):
                     src = lax.rem(mine + e, SIDE)
                     pltpu.make_async_copy(came.at[item, src], in_buf.at[slot, src], load_sem.at[slot]).start()
 
-    def first(item, _):
-        start(0, 0, item)
-        return 0
-
-    lax.fori_loop(0, n_items, first, 0)
+    weights = [pltpu.make_async_copy(src, dst, weight_sem.at[i]) for i, (src, dst) in enumerate(((w1_hbm, w1), (w3_hbm, w3), (w2_hbm, w2)))]
+    for copy in weights:
+        copy.start()
+
+    n_tok, d_model = toks.shape
+    per_item = SIDE**3 * UNIT
+
+    def first(t, _):
+        @pl.when(t < n_items)
+        def _():
+            row_nums = lax.broadcasted_iota(jnp.int32, (n_tok, per_item), 1) + t * per_item
+            sel = jnp.zeros((n_tok, per_item), jnp.float32)
+            for j in range(dest.shape[1]):
+                sel = jnp.where(dest[:, j : j + 1] == row_nums, 1.0, sel)
+            res = lax.dot_general(sel.astype(jnp.bfloat16), toks[...], (((0,), (0,)), ((), ())), preferred_element_type=jnp.float32)
+            out_buf[t] = res.reshape(SIDE, SIDE, SIDE, UNIT, d_model).astype(jnp.bfloat16)
+
+        @pl.when(t > 0)
+        def _():
+            start(0, 0, t - 1)
+
+        return 0
+
+    lax.fori_loop(0, n_items + 1, first, 0)
+    for copy in weights:
+        copy.wait()
 
     def at_step(t, lag, act):
         item = t - lag
@@ -148,7 +164,6 @@
         @pl.when(busy)
         def _():
             slot = lax.rem(now, 2)
-            d_model = in_buf.shape[-1]
             pltpu.make_async_copy(came.at[now], in_buf.at[slot], load_sem.at[slot]).wait()
             x = in_buf[slot].astype(jnp.float32).reshape(SIDE**3 * UNIT, d_model).astype(jnp.bfloat16)
             gate = jnp.dot(x, w1[...], preferred_element_type=jnp.float32)
@@ -214,35 +229,34 @@
         dest = jnp.where(kept, (item * n_exp + place) * UNIT + slot_ids % UNIT, -1)
         row_nums = jnp.arange(n_rows, dtype=jnp.int32)
         weights = jnp.zeros((n_tok, n_rows), jnp.float32)
-        sel = jnp.zeros((n_tok, n_rows), jnp.bool_)
         for j in range(top_k):
-            here = dest[:, j : j + 1] == row_nums[None, :]
-            sel = sel | here
-            weights = weights + jnp.where(here, gate_vals[:, j : j + 1], 0.0)
+            weights = weights + jnp.where(dest[:, j : j + 1] == row_nums[None, :], gate_vals[:, j : j + 1], 0.0)
         weights = lax.optimization_barrier(jnp.concatenate(bf16_parts(weights), axis=0))
 
         boxes = (n_items, SIDE, SIDE, SIDE, UNIT, d_model)
-        packed = lax.dot_general(sel.astype(jnp.bfloat16), tokens, (((0,), (0,)), ((), ())), preferred_element_type=jnp.float32)
-        packed = packed.astype(jnp.bfloat16).reshape(boxes)
         vmem = pl.BlockSpec(memory_space=pltpu.VMEM)
         hbm = pl.BlockSpec(memory_space=pl.ANY)
         back = pl.pallas_call(
             functools.partial(expert_kernel, n_items),
             name="expert_exchange",
             out_shape=[jax.ShapeDtypeStruct(boxes, jnp.bfloat16)] * 6,
-            in_specs=[hbm, vmem, vmem, vmem],
+            in_specs=[vmem, vmem, hbm, hbm, hbm],
             out_specs=[hbm] * 6,
             scratch_shapes=[
                 pltpu.VMEM((2,) + boxes[1:], jnp.bfloat16),
                 pltpu.VMEM(boxes, jnp.bfloat16),
+                pltpu.VMEM((d_model, d_ff), jnp.bfloat16),
+                pltpu.VMEM((d_model, d_ff), jnp.bfloat16),
+                pltpu.VMEM((d_ff, d_model), jnp.bfloat16),
                 pltpu.SemaphoreType.DMA((2,)),
                 pltpu.SemaphoreType.DMA((2, n_items, 3, 3)),
                 pltpu.SemaphoreType.DMA((2, n_items, 3, 3)),
                 pltpu.SemaphoreType.DMA((2, n_items, 3)),
+                pltpu.SemaphoreType.DMA((3,)),
             ],
             compiler_params=pltpu.CompilerParams(has_side_effects=True, vmem_limit_bytes=66_000_000),
             cost_estimate=pl.CostEstimate(flops=6 * n_rows * d_model * d_ff, bytes_accessed=n_rows * d_model * 6, transcendentals=n_rows * d_ff),
-        )(packed, expert_w1[0], expert_w3[0], expert_w2[0])[5].reshape(n_rows, d_model)
+        )(tokens, dest, expert_w1[0], expert_w3[0], expert_w2[0])[5].reshape(n_rows, d_model)
         routed = jnp.dot(weights, back, preferred_element_type=jnp.float32)
         routed = routed[:n_tok] + routed[n_tok : 2 * n_tok] + routed[2 * n_tok :]
         return (tokens.astype(jnp.float32) + shared_out + routed).astype(jnp.bfloat16)

time: 494 us -> 485 us (0.982)
  matrix products: 42.3 us -> 31.6 us
    dot_general x1 -> x0, matrix products: 12.1 us -> none  [layer_body(): lax.dot_general(sel.astype(jnp.bfloat16), tokens, (((0,), (0,)), ((), ())...]
  transfers between devices with their start and end apart: 2 -> 2, of which waited for: 0 -> 0; matrix products, arithmetic and copies ran while one was open for 8% -> 6% of each run, Pallas kernels for 88% -> 89%
where the time goes in v3:
time: 485 us
  Pallas kernels  431 us (89%)
  matrix products  31.6 us (7%)
  other arithmetic  11.1 us (2%)
  starting transfers between devices  5.69 us (1%)
  local copies, waits for them, and re-layouts  5.29 us (1%)
    pallas_call x1, Pallas kernels, layer_body(): pl.pallas_call(functools.partial(expert_kernel, n_items), name='expert_ex...  431 us
    dot_general x1, matrix products, layer_body(): routed = jnp.dot(weights, back, preferred_element_type=jnp.float32)  15.7 us
    dot_general x1, matrix products, swiglu(): return jnp.dot(hidden, w2, preferred_element_type=jnp.float32)  10.5 us
  transfers between devices with their start and end apart: 2, of which 0 were waited for; matrix products, arithmetic and copies ran while one was open for 6% of the time, Pallas kernels for 89%

profile of v3, /device:TPU:1, one launch (start us, length us, event | category | flops | bytes accessed | tf_op | source)
XLA Modules:
  0.0 484.8 jit_solution(7234617992277016822)
XLA Ops:
  0.0 1.4 collective-permute-start
  1.4 0.8 copy.39
  2.2 0.7 broadcast_compare_fusion
  2.9 0.8 copy.46
  3.7 0.9 select_reduce_fusion
  4.6 0.1 copy.40
  4.7 0.2 copy.41
  4.8 0.4 fusion.10.dest
  5.2 0.0 copy-start
  5.2 0.4 slice_reduce_fusion.5
  5.7 0.9 fusion.15
  6.6 431.0 %expert_exchange.1 = (bf16[9,4,4,4,8,2048]{5,4,3,2,1,0:T(8,128)(2,1)}, bf16[9,4,4,4,8,2048]{5,4,3,2,1,0:T(8,128)(2,1)}, bf16[9,4,4,4,8,2048]{5,4,3,2,1,0:T(8,128...) custom-call(bf16[192,2048]{1,0:T(8,128)(2,1)} %toks.1, ...), custom_call_target="tpu_custom_call" | custom-call | flops 79725330432 | bytes 56623104 | tf_op jit(solution)/shard_map/expert_exchange/pallas_call | solution.py:239
  437.6 0.0 slice-start
  437.6 4.6 reduce-precision_convert_fusion.1
  442.2 0.0 slice-start.1
  442.2 2.8 pad_maximum_fusion
  445.0 0.9 constant_dynamic-update-slice_fusion.1
  445.9 1.0 constant_dynamic-update-slice_fusion
  446.9 5.4 %fusion.18 = f32[384,1408]{1,0:T(8,128)} fusion(bf16[384,2048]{1,0:T(8,128)(2,1)} %constant_dynamic-update-slice_fusion, bf16[2048,1408]{1,0:T(8,128)(2,1)S(1)} %bitcast.29), kind=kOutput, calls=%fused_computation.64 | convolution fusion | flops 2214592512 | bytes 9502720 | tf_op jit(solution)/shard_map/dot_general | solution.py:22
  452.4 10.5 %fusion.5 = f32[384,2048]{1,0:T(8,128)S(1)} fusion(bf16[1408,2048]{1,0:T(8,128)(2,1)} %param.18, f32[384,1408]{1,0:T(8,128)} %fusion.18, bf16[384,2048]{1,0:T(8,128)(2,1)} %constant_dynamic-update-slice_fusion, bf16[2048,1408]{1,0:T(8,128)(2,1)} %param.17), kind=kOutput, calls=%fused_computation.21 | convolution fusion | flops 4432429056 | bytes 18415616 | tf_op jit(solution)/shard_map/dot_general | solution.py:25
  462.8 0.1 slice.69
  463.0 4.3 collective-permute-start.1
  467.3 15.7 %fusion.19 = f32[576,2048]{1,0:T(8,128)S(1)} fusion(bf16[576,4608]{1,0:T(8,128)(2,1)} %pad_maximum_fusion, bf16[4608,2048]{1,0:T(8,128)(2,1)} %bitcast.30), kind=kOutput, calls=%fused_computation.65 | convolution fusion | flops 10871635968 | bytes 28901376 | tf_op jit(solution)/shard_map/dot_general | solution.py:260
  483.0 1.8 fusion.3
  (10 shorter events, 0.0 us)
Async XLA Ops:
  0.0 445.9 %collective-permute-start = (bf16[192,2048]{1,0:T(8,128)(2,1)}, bf16[192,2048]{1,0:T(8,128)(2,1)S(1)}, u32[]{:S(2)}, u32[]{:S(2)}) collective-permute-start(bf16[192,2048]{1,0:T(8,128)(2,1)} %toks.1), channel_id=1, source_target_pairs={{0,64},{64,0},{1,65},{65,1},{2,66},{66,2},{3,67},{67,3},{4,68},{68... | collective-permute-start | bytes 2359304 | tf_op jit(solution)/shard_map/ppermute | solution.py:221
  5.2 1.4 copy-start
  437.6 9.3 %slice-start = ((s8[5767168]{0:T(1024)(128)(4,1)}), s8[4194304]{0:T(1024)(128)(4,1)S(1)}, s32[]{:S(2)}) async-start(s8[5767168]{0:T(1024)(128)(4,1)} %bitcast.28), calls=%async_computation | async-start | bytes 8388608
  442.2 2.8 copy-start.1
  442.2 4.7 slice-start.1
  463.0 20.0 %collective-permute-start.1 = (f32[192,2048]{1,0:T(8,128)S(1)}, f32[192,2048]{1,0:T(8,128)S(1)}, u32[]{:S(2)}, u32[]{:S(2)}) collective-permute-start(f32[192,2048]{1,0:T(8,128)S(1)} %slice.69), channel_id=1, source_target_pairs={{0,64},{64,0},{1,65},{65,1},{2,66},{66,2},{3,67},{67,3},{4,68},{68... | collective-permute-start | bytes 4718600 | tf_op jit(solution)/shard_map/ppermute | solution.py:223
  467.3 15.7 %copy-start.2 = (bf16[192,2048]{1,0:T(8,128)(2,1)S(1)}, bf16[192,2048]{1,0:T(8,128)(2,1)}, u32[]{:S(2)}) copy-start(bf16[192,2048]{1,0:T(8,128)(2,1)} %toks.1) | copy-start | bytes 2359300
